TPU v7x, 32 devices: a whole 2x2x4 slice. The times are simulated.
32 devices in a mesh: grp: 8 (over z, core), sub: 4 (over y, x).
Axes of the slice: x: 2, y: 2, z: 4, core: 2. Of those that a mesh axis runs over, the one named last changes fastest.
Arguments:
- coarse_op: float32 [256, 64, 576], P(('grp', 'sub'))
- right_side: float32 [256, 64, 64], P(('grp', 'sub')), may hold values from -6 to 6
- owner_map: int32 [256], replicated, may hold values from 0 to 255, as said below
- neighbor_table: int32 [256, 8], replicated, may hold values from 0 to 255, as said below
Outputs:
- solution: float32 [256, 64, 64], P(('grp', 'sub'))
Inputs may be any that keep to these rules, and one draw needn't show every extreme that they name: `owner_map`: a permutation of 0 .. 255. `neighbor_table`: row t lists the neighbours of coarse site t on a periodic 4^4 lattice in the order +x, -x, +y, -y, +z, -z, +t, -t; lattice positions carry the site numbers in a permuted order.
All inputs are finite; a program needn't handle non-finite values.
Results may differ from a plain program's by a relative error of at most 0.0001.
Values sent between devices are 32-bit elements; how exact they have to be, the bound alone decides.
A program may use at most 64 MiB of HBM per device.

v0:
```python
import jax
import jax.numpy as jnp
from jax import lax
from jax.sharding import PartitionSpec as P

ITERS = 3


def inner_product(first, second):
    return jnp.sum(first * second, axis=(0, 1))


def per_device(coarse_op, right_side, owner_map, neighbor_table):
    n_sub = lax.axis_size("sub")
    n_grp = lax.axis_size("grp")
    per_dev = coarse_op.shape[0]
    dof_count = coarse_op.shape[1]
    site_count = owner_map.shape[0]
    site_ids = jnp.arange(site_count, dtype=jnp.int32)
    inverse = jnp.sum(
        jnp.where(owner_map[None, :] == site_ids[:, None], site_ids[None, :], 0), axis=1
    )
    link = inverse[neighbor_table[owner_map]]
    op_rows = lax.all_gather(coarse_op, "grp", axis=0, tiled=True)
    rhs_rows = lax.all_to_all(right_side, "grp", split_axis=2, concat_axis=0, tiled=True)

    def reduce_sum(values):
        return lax.psum(values, "sub")

    row_count = op_rows.shape[0]
    local_rows = jnp.arange(row_count, dtype=jnp.int32)
    own_slots = (
        local_rows // per_dev * n_sub + lax.axis_index("sub")
    ) * per_dev + local_rows % per_dev
    target = link[own_slots]
    target_block = target // per_dev
    position = (target_block % n_sub * n_grp + target_block // n_sub) * per_dev + target % per_dev
    rhs_count = rhs_rows.shape[2]
    beta = jnp.sqrt(reduce_sum(inner_product(rhs_rows, rhs_rows)))
    krylov = [rhs_rows / beta]
    hess = jnp.zeros((ITERS + 1, ITERS, rhs_count), jnp.float32)
    for column in range(ITERS):
        apply_vector = krylov[column]
        piece = lax.all_gather(apply_vector, "sub", axis=0, tiled=True)
        count = piece.shape[0]
        select = (position[:, :, None] == jnp.arange(count, dtype=jnp.int32)[None, None, :]).astype(
            jnp.float32
        )
        nearby = jnp.einsum("lkr,rab->lkab", select, piece, precision=lax.Precision.HIGHEST)
        stacked = jnp.concatenate([apply_vector[:, None], nearby], axis=1).reshape(
            row_count, 9 * dof_count, rhs_count
        )
        image = jnp.einsum("sac,scr->sar", op_rows, stacked, precision=lax.Precision.HIGHEST)
        for index_i in range(column + 1):
            coeff = reduce_sum(inner_product(krylov[index_i], image))
            image = image - coeff * krylov[index_i]
            hess = hess.at[index_i, column].set(coeff)
        norm_sq = reduce_sum(inner_product(image, image))
        norm_value = jnp.sqrt(norm_sq)
        hess = hess.at[column + 1, column].set(norm_value)
        krylov.append(image / norm_value)
    gram_matrix = jnp.einsum("ijr,ikr->rjk", hess, hess, precision=lax.Precision.HIGHEST)
    projected = (beta[None, :] * hess[0]).T
    factor = jnp.linalg.cholesky(gram_matrix)
    halfway = jax.scipy.linalg.solve_triangular(factor, projected[..., None], lower=True)
    weights = jax.scipy.linalg.solve_triangular(factor, halfway, lower=True, trans=1)[..., 0]
    solution = jnp.zeros_like(rhs_rows)
    for column in range(ITERS):
        solution = solution + weights[:, column][None, None, :] * krylov[column]
    return lax.all_to_all(solution, "grp", split_axis=0, concat_axis=2, tiled=True)


def solution(mesh):
    placed = (P(("grp", "sub"), None, None), P(("grp", "sub"), None, None), P(), P())
    return jax.shard_map(
        per_device,
        mesh=mesh,
        in_specs=placed,
        out_specs=P(("grp", "sub"), None, None),
        check_vma=False,
    )
```

profile of v0, /device:TPU:0, one launch (start us, length us, event | category | flops | bytes accessed | tf_op | source)
XLA Modules:
  0.0 307.9 jit_solution(5895258015328376698)
XLA Ops:
  9.2 6.4 %all-to-all-start = ((f32[8,1,4096]{2,1,0:T(1,128)}), f32[8,1,4096]{2,1,0:T(1,128)S(1)}, u32[]{:S(2)}, u32[]{:S(2)}) async-start(f32[8,1,4096]{2,1,0:T(1,128)} %reshape.534), calls=%async_computation | async-start | bytes 262144 | tf_op jit(solution)/shard_map/all_to_all | solution.py:25
  16.7 13.1 %gather_fusion.1 = s32[2048]{0:T(1024)S(1)} fusion(s32[256]{0:T(256)S(1)} %select_reduce_fusion, s32[2048]{0:T(1024)S(1)} %broadcast_clamp_fusion), kind=kCustom, calls=%fused_computation.1 | custom fusion | bytes 24576 | tf_op jit(solution)/shard_map/gather | solution.py:23
  32.4 9.9 %psum.70 = f32[8]{0:T(128)S(1)} all-reduce(f32[8]{0:T(128)S(1)} %fusion.13), channel_id=1, replica_groups=mesh['grp'=8,'sub'=4] {'sub'}, use_global_device_ids=true, to_apply=%region_1.2 | all-reduce | flops 8 | bytes 64 | tf_op jit(solution)/shard_map/psum | solution.py:28
  42.5 11.9 %all_gather.12 = f32[256,64,8]{1,0,2:T(8,128)S(1)} all-gather(f32[64,64,8]{1,0,2:T(8,128)S(1)} %bitcast_divide_fusion), channel_id=1, replica_groups=mesh['grp'=8,'sub'=4] {'sub'}, dimensions={0}, use_global_device_ids=true | all-gather | bytes 655360 | tf_op jit(solution)/shard_map/all_gather | solution.py:44
  55.8 2.9 pad_maximum_fusion
  58.7 4.3 %copy.148 = f32[64,9,64,8]{0,3,2,1:T(8,128)S(1)} copy(f32[64,9,64,8]{2,1,3,0:T(8,128)} %pad_maximum_fusion) | data formatting | bytes 2359296 | tf_op jit(solution)/shard_map/concatenate | solution.py:50
  65.0 46.1 %all-gather.2.cloned.1.call-done = f32[64,64,576]{2,1,0:T(8,128)} async-done(((f32[8,64,576]{2,1,0:T(8,128)}), f32[64,64,576]{2,1,0:T(8,128)}) %all-gather.2.cloned.1.call-update) | async-done | bytes 9437200 | tf_op jit(solution)/shard_map/all_gather | solution.py:24
  111.1 13.0 %fusion.38 = f32[64,8,64]{2,1,0:T(8,128)S(1)} fusion(f32[64,576,8]{1,2,0:T(8,128)} %copy.149, f32[64,64,576]{2,1,0:T(8,128)} %all-gather.2.cloned.1.call-done), kind=kOutput, calls=%fused_computation.107 | convolution fusion | flops 226492416 | bytes 10747904 | tf_op jit(solution)/shard_map/sac,scr->sar/dot_general | solution.py:53
  124.3 9.8 %psum.71 = f32[8]{0:T(128)S(1)} all-reduce(f32[8]{0:T(128)S(1)} %fusion.12), channel_id=1, replica_groups=mesh['grp'=8,'sub'=4] {'sub'}, use_global_device_ids=true, to_apply=%region_4.5 | all-reduce | flops 8 | bytes 64 | tf_op jit(solution)/shard_map/psum | solution.py:28
  134.4 8.0 %psum.72 = f32[8]{0:T(128)S(1)} all-reduce(f32[8]{0:T(128)S(1)} %multiply_reduce_fusion.5), channel_id=1, replica_groups=mesh['grp'=8,'sub'=4] {'sub'}, use_global_device_ids=true, to_apply=%region_6.7 | all-reduce | flops 8 | bytes 64 | tf_op jit(solution)/shard_map/psum | solution.py:28
  142.5 13.0 %all_gather.14 = f32[256,64,8]{1,0,2:T(8,128)S(1)} all-gather(f32[64,64,8]{1,0,2:T(8,128)S(1)} %broadcast_divide_fusion.2), channel_id=1, replica_groups=mesh['grp'=8,'sub'=4] {'sub'}, dimensions={0}, use_global_device_ids=true | all-gather | bytes 655360 | tf_op jit(solution)/shard_map/all_gather | solution.py:44
  159.7 4.3 %copy.152 = f32[64,9,64,8]{0,3,2,1:T(8,128)S(1)} copy(f32[64,9,64,8]{2,1,3,0:T(8,128)} %pad_maximum_fusion.1) | data formatting | bytes 2359296 | tf_op jit(solution)/shard_map/concatenate | solution.py:50
  166.1 13.0 %fusion.39 = f32[64,8,64]{2,1,0:T(8,128)S(1)} fusion(f32[64,576,8]{1,2,0:T(8,128)} %copy.153, f32[64,64,576]{2,1,0:T(8,128)} %all-gather.2.cloned.1.call-done), kind=kOutput, calls=%fused_computation.108 | convolution fusion | flops 226492416 | bytes 10747904 | tf_op jit(solution)/shard_map/sac,scr->sar/dot_general | solution.py:53
  180.0 8.9 %psum.73 = f32[8]{0:T(128)S(1)} all-reduce(f32[8]{0:T(128)S(1)} %fusion.11), channel_id=1, replica_groups=mesh['grp'=8,'sub'=4] {'sub'}, use_global_device_ids=true, to_apply=%region_8.9 | all-reduce | flops 8 | bytes 64 | tf_op jit(solution)/shard_map/psum | solution.py:28
  189.2 8.7 %psum.74 = f32[8]{0:T(128)S(1)} all-reduce(f32[8]{0:T(128)S(1)} %get-tuple-element.115), channel_id=1, replica_groups=mesh['grp'=8,'sub'=4] {'sub'}, use_global_device_ids=true, to_apply=%region_10.11 | all-reduce | flops 8 | bytes 64 | tf_op jit(solution)/shard_map/psum | solution.py:28
  198.8 9.0 %psum.75 = f32[8]{0:T(128)S(1)} all-reduce(f32[8]{0:T(128)S(1)} %multiply_reduce_fusion.3), channel_id=1, replica_groups=mesh['grp'=8,'sub'=4] {'sub'}, use_global_device_ids=true, to_apply=%region_12.13 | all-reduce | flops 8 | bytes 64 | tf_op jit(solution)/shard_map/psum | solution.py:28
  207.9 11.6 %all_gather.15 = f32[256,64,8]{1,0,2:T(8,128)S(1)} all-gather(f32[64,64,8]{1,0,2:T(8,128)S(1)} %broadcast_divide_fusion.1), channel_id=1, replica_groups=mesh['grp'=8,'sub'=4] {'sub'}, dimensions={0}, use_global_device_ids=true | all-gather | bytes 655360 | tf_op jit(solution)/shard_map/all_gather | solution.py:44
  223.7 4.3 %copy.156 = f32[64,9,64,8]{0,3,2,1:T(8,128)S(1)} copy(f32[64,9,64,8]{2,1,3,0:T(8,128)} %pad_maximum_fusion.2) | data formatting | bytes 2359296 | tf_op jit(solution)/shard_map/concatenate | solution.py:50
  230.0 13.0 %fusion.40 = f32[64,8,64]{2,1,0:T(8,128)S(1)} fusion(f32[64,576,8]{1,2,0:T(8,128)} %copy.157, f32[64,64,576]{2,1,0:T(8,128)} %all-gather.2.cloned.1.call-done), kind=kOutput, calls=%fused_computation.109 | convolution fusion | flops 226492416 | bytes 10747904 | tf_op jit(solution)/shard_map/sac,scr->sar/dot_general | solution.py:53
  243.9 8.9 %psum.76 = f32[8]{0:T(128)S(1)} all-reduce(f32[8]{0:T(128)S(1)} %fusion.10), channel_id=1, replica_groups=mesh['grp'=8,'sub'=4] {'sub'}, use_global_device_ids=true, to_apply=%region_15.16 | all-reduce | flops 8 | bytes 64 | tf_op jit(solution)/shard_map/psum | solution.py:28
  253.0 8.7 %psum.77 = f32[8]{0:T(128)S(1)} all-reduce(f32[8]{0:T(128)S(1)} %get-tuple-element.113), channel_id=1, replica_groups=mesh['grp'=8,'sub'=4] {'sub'}, use_global_device_ids=true, to_apply=%region_17.18 | all-reduce | flops 8 | bytes 64 | tf_op jit(solution)/shard_map/psum | solution.py:28
  262.0 8.9 %psum.78 = f32[8]{0:T(128)S(1)} all-reduce(f32[8]{0:T(128)S(1)} %multiply_reduce_fusion.1), channel_id=1, replica_groups=mesh['grp'=8,'sub'=4] {'sub'}, use_global_device_ids=true, to_apply=%region_19.20 | all-reduce | flops 8 | bytes 64 | tf_op jit(solution)/shard_map/psum | solution.py:28
  271.1 8.1 %psum.79 = f32[8]{0:T(128)S(1)} all-reduce(f32[8]{0:T(128)S(1)} %multiply_reduce_fusion), channel_id=1, replica_groups=mesh['grp'=8,'sub'=4] {'sub'}, use_global_device_ids=true, to_apply=%region_21.22 | all-reduce | flops 8 | bytes 64 | tf_op jit(solution)/shard_map/psum | solution.py:28
  290.0 9.1 %all_to_all.39 = f32[8,1,4096]{2,1,0:T(1,128)S(1)} all-to-all(f32[8,1,4096]{2,1,0:T(1,128)S(1)} %reshape.536), channel_id=1, replica_groups=mesh['grp'=8,'sub'=4] {'grp'}, dimensions={0} | all-to-all | bytes 262144 | tf_op jit(solution)/shard_map/all_to_all | solution.py:70
  (96 shorter events, 39.2 us)
Async XLA Ops:
  6.5 9.0 %copy-start = (s32[256,8]{0,1:T(8,128)S(1)}, s32[256,8]{0,1:T(8,128)}, u32[]{:S(2)}) copy-start(s32[256,8]{0,1:T(8,128)} %param.25) | copy-start | bytes 24580
  6.5 9.2 %copy-start.1 = (s32[256]{0:T(256)S(1)}, s32[256]{0:T(256)}, u32[]{:S(2)}) copy-start(s32[256]{0:T(256)} %param.24) | copy-start | bytes 3076
  6.5 104.6 %all-gather.2.cloned.1.call-start = ((), (), s32[]{:S(2)}) async-start(), calls=%async_computation.2 | async-start | bytes 11796480 | tf_op jit(solution)/shard_map/all_gather | solution.py:24
  9.2 21.4 %all-to-all-start = ((f32[8,1,4096]{2,1,0:T(1,128)}), f32[8,1,4096]{2,1,0:T(1,128)S(1)}, u32[]{:S(2)}, u32[]{:S(2)}) async-start(f32[8,1,4096]{2,1,0:T(1,128)} %reshape.534), calls=%async_computation | async-start | bytes 262144 | tf_op jit(solution)/shard_map/all_to_all | solution.py:25
  166.1 13.2 %copy-start.2 = (s32[3]{0:T(128)S(1)}, s32[3]{0:T(128)}, u32[]{:S(2)}) copy-start(s32[3]{0:T(128)} %constant.393.clone.1) | copy-start | bytes 40
Sparse Core Ops, SparseCore 0:
  9.0 102.0 all-gather.1
where the time goes:
time: 309 us; the launch traced here: 308 us
  blocking collectives  135 us (44%)
  waiting for transfers between devices  46.8 us (15%)
  local copies, waits for them, and re-layouts  42.9 us (14%)
  matrix products  42.5 us (14%)
  other arithmetic  21.1 us (7%)
  between operations  13.7 us (4%)
  starting transfers between devices  6.36 us (2%)
    psum x10, blocking collectives, reduce_sum(): return lax.psum(values, 'sub')  89 us
    all_gather x1, waiting for transfers between devices, per_device(): op_rows = lax.all_gather(coarse_op, 'grp', axis=0, tiled=True)  46.1 us
    dot_general x3, matrix products, per_device(): jnp.einsum('sac,scr->sar', op_rows, stacked, precision=lax.Precision.HIGH...  38.9 us
    all_gather x3, blocking collectives, per_device(): piece = lax.all_gather(apply_vector, 'sub', axis=0, tiled=True)  36.5 us
    gather x3, local copies, waits for them, and re-layouts, per_device(): link = inverse[neighbor_table[owner_map]]  14 us
    concatenate x3, local copies, waits for them, and re-layouts, per_device(): jnp.concatenate([apply_vector[:, None], nearby], axis=1)  13 us
    all_to_all x1, blocking collectives, per_device(): lax.all_to_all(solution, 'grp', split_axis=0, concat_axis=2, tiled=True)  9.14 us
    concatenate x3, other arithmetic, per_device(): jnp.concatenate([apply_vector[:, None], nearby], axis=1)  8.55 us
  transfers between devices with their start and end apart: 2, of which 1 were waited for; matrix products, arithmetic and copies ran while one was open for 10% of the time, Pallas kernels for 0%

commit v1 on v0

v1 whole, which is shorter than its diff:
```python
import functools
import math

import jax
import jax.numpy as jnp
from jax import lax
from jax.experimental import pallas as pl
from jax.experimental.pallas import tpu as pltpu
from jax.sharding import PartitionSpec as P

LANES = 128
MESH = pl.DeviceIdType.MESH
F32 = jnp.float32
BF16 = jnp.bfloat16


def ring_order(count):
    side = math.isqrt(count)
    if side * side != count or side % 2:
        return list(range(count))
    order = list(range(side))
    for row in range(1, side):
        columns = range(side - 1, 0, -1) if row % 2 else range(1, side)
        order += [row * side + column for column in columns]
    return order + [row * side for row in range(side - 1, 0, -1)]


def lookup(table, index):
    found = jnp.int32(table[0])
    for place in range(1, len(table)):
        found = jnp.where(index == place, jnp.int32(table[place]), found)
    return found


def split(value):
    high = value.astype(BF16)
    return high, (value - high.astype(F32)).astype(BF16)


def kernel(
    planes, subs, per_dev, dof, half, hops,
    place_ref, table_ref, owner_ref, rhs_ref, op_ref, out_ref,
    vec0, vec1, vec2, image_ref, op_other, cp_high, cp_low, links, parts, sent, received,
    z_send, z_recv, r_send, r_recv, p_send, p_recv, s_send, s_recv, local_sem,
):
    pack = LANES // half
    rows = dof // pack
    block = 2 * per_dev
    chips = planes * subs
    sites = chips * block
    grp, sub = lax.axis_index("grp"), lax.axis_index("sub")
    plane, core = grp // 2, grp % 2
    partner = (plane * 2 + (1 - core), sub)
    me = plane * subs + sub
    order = ring_order(subs)
    where_in_ring = [order.index(s) for s in range(subs)]
    ring_pos = lookup(where_in_ring, sub)

    def ring_sub(offset):
        return lookup(order, lax.rem(ring_pos + offset + subs, subs))

    right, left = ring_sub(1), ring_sub(-1)

    def chip_device(chip):
        return (chip // subs * 2 + core, lax.rem(chip, subs))

    barrier = pltpu.get_barrier_semaphore()
    pl.semaphore_signal(barrier, inc=1, device_id=partner, device_id_type=MESH)

    @pl.loop(1, chips)
    def _(step):
        pl.semaphore_signal(
            barrier, inc=1, device_id=chip_device(lax.rem(me + step, chips)), device_id_type=MESH
        )

    pl.semaphore_wait(barrier, chips)

    def remote(src, dst, send, recv, device):
        return pltpu.make_async_remote_copy(
            src_ref=src, dst_ref=dst, send_sem=send, recv_sem=recv, device_id=device, device_id_type=MESH
        )

    own_rows = pl.ds(me * block + core * per_dev, per_dev)
    other_rows = pl.ds(me * block + (1 - core) * per_dev, per_dev)
    rhs_swap = remote(rhs_ref.at[1 - core], vec0.at[own_rows], p_send.at[0], p_recv.at[0], partner)
    rhs_swap.start()
    op_swap = remote(op_ref, op_other, p_send.at[1], p_recv.at[1], partner)
    op_swap.start()
    rhs_keep = pltpu.make_async_copy(rhs_ref.at[core], vec0.at[own_rows], local_sem)
    rhs_keep.start()
    rhs_keep.wait()
    rhs_swap.wait()

    full_steps = (subs - 1) // 2
    ring_steps = subs // 2
    keys = [(0, 0)] + [(way, dist) for dist in range(1, planes) for way in (0, 1)]

    def gather(number, vec, meanwhile=None):
        def at(chip_plane, chip_sub, piece=None):
            start = (chip_plane * subs + chip_sub) * block
            if piece is None:
                return vec.at[pl.ds(start, block)]
            return vec.at[pl.ds(start + piece * per_dev, per_dev)]

        def plane_of(key):
            way, dist = key
            return plane - dist if way == 0 else plane + dist

        def present(key):
            way, dist = key
            return plane >= dist if way == 0 else plane + dist < planes

        def guarded(key, action):
            if key[1] == 0:
                action()
            else:
                pl.when(present(key))(action)

        def z_copy(way, dist):
            src_plane = plane - (dist - 1) if way == 0 else plane + (dist - 1)
            next_plane = plane + 1 if way == 0 else plane - 1
            ref = at(src_plane, sub)
            return remote(
                ref, ref, z_send.at[number, way, dist], z_recv.at[number, way, dist],
                (next_plane * 2 + core, sub),
            )

        def z_goes(way):
            return plane < planes - 1 if way == 0 else plane > 0

        def z_arrival(key):
            way, dist = key
            ref = at(plane_of(key), sub)
            return remote(
                ref, ref, z_send.at[number, way, dist], z_recv.at[number, way, dist], (grp, sub)
            )

        def ring_copy(key, way, step, arriving):
            offset = step if arriving else step - 1
            src = ring_sub(-offset if way == 0 else offset)
            piece = way if 2 * step == subs else None
            ref = at(plane_of(key), src, piece)
            index = keys.index(key)
            return remote(
                ref, ref, r_send.at[number, index, way, step], r_recv.at[number, index, way, step],
                (grp, right if way == 0 else left),
            )

        def z_forward(way, dist):
            if dist < planes:
                pl.when(z_goes(way))(lambda: z_copy(way, dist).start())

        def ring_start(key, step):
            if step <= ring_steps:
                for way in (0, 1):
                    ring_copy(key, way, step, False).start()

        def ring_follow(key):
            for step in range(1, ring_steps):
                for way in (0, 1):
                    ring_copy(key, way, step, True).wait_recv()
                    ring_copy(key, way, step + 1, False).start()

        def ring_last(key):
            if ring_steps:
                for way in (0, 1):
                    ring_copy(key, way, ring_steps, True).wait_recv()

        def arrive(key):
            def action():
                z_arrival(key).wait_recv()
                z_forward(key[0], key[1] + 1)
                ring_start(key, 1)

            guarded(key, action)

        for way in (0, 1):
            z_forward(way, 1)
        ring_start((0, 0), 1)
        if meanwhile is not None:
            meanwhile[0]()
        behind = [(0, 0)]
        for dist in range(1, planes):
            now = [key for key in keys if key[1] == dist]
            for key in now:
                arrive(key)
            for key in behind:
                guarded(key, functools.partial(ring_follow, key))
            behind = now
            if meanwhile is not None and dist < len(meanwhile):
                meanwhile[dist]()
        for key in behind:
            guarded(key, functools.partial(ring_follow, key))
        for key in keys:
            guarded(key, functools.partial(ring_last, key))

        for dist in range(1, planes):
            for way in (0, 1):
                goes = jnp.logical_and(z_goes(way), present((way, dist - 1)))
                pl.when(goes)(lambda way=way, dist=dist: z_copy(way, dist).wait_send())

        def ring_sends(key):
            for step in range(1, ring_steps + 1):
                for way in (0, 1):
                    ring_copy(key, way, step, False).wait_send()

        for key in keys:
            guarded(key, functools.partial(ring_sends, key))

    width = (hops + 1) * dof
    depth = (hops + 1) * rows

    def regroup(source, first):
        high, low = split(source[...].reshape(per_dev * dof, width))
        at_row = lax.broadcasted_iota(jnp.int32, (width, depth), 0)
        at_column = lax.broadcasted_iota(jnp.int32, (width, depth), 1)
        for quarter in range(pack):
            wanted = at_column // rows * dof + quarter * rows + at_column % rows
            pick = jnp.where(at_row == wanted, 1.0, 0.0).astype(F32).astype(BF16)
            for value, kept in ((high, cp_high), (low, cp_low)):
                moved = jnp.dot(value, pick, preferred_element_type=F32).astype(BF16)
                kept[first : first + per_dev, quarter * dof : (quarter + 1) * dof, :] = moved.reshape(
                    per_dev, dof, depth
                )

    def find_links():
        @pl.loop(0, per_dev)
        def _(local):
            for side in (0, 1):
                slot_grp = plane * 2 + (core if side == 0 else 1 - core)
                slot = (slot_grp * subs + sub) * per_dev + local
                coarse = owner_ref[slot]
                for hop in range(hops):
                    links[(side * per_dev + local) * hops + hop] = place_ref[table_ref[coarse * hops + hop]]

    def prepare():
        find_links()
        regroup(op_ref, 0)

    def prepare_other():
        op_swap.wait()
        regroup(op_other, per_dev)

    lane_group = lax.broadcasted_iota(jnp.int32, (rows, LANES), 1) // half

    def apply_op(vec, over, store):
        def one(index, base, count_row):
            own = me * block + count_row
            pieces = [vec[own]] + [vec[links[index * hops + hop]] for hop in range(hops)]
            high, low = split(jnp.concatenate(pieces, axis=0))
            both = jnp.concatenate([high, low], axis=1)
            first = jnp.dot(cp_high[index], both, preferred_element_type=F32)
            second = jnp.dot(cp_low[index], high, preferred_element_type=F32)
            product = first[:, :LANES] + first[:, LANES:] + second
            total = None
            for turn in range(pack):
                picked = None
                for quarter in range(pack):
                    start = quarter * dof + (quarter + turn) % pack * rows
                    term = product[start : start + rows]
                    picked = term if picked is None else jnp.where(lane_group == quarter, term, picked)
                if turn:
                    picked = pltpu.roll(picked, turn * half, 1)
                total = picked if total is None else total + picked
            store(count_row, total / over)

        for side in (0, 1):
            base = (core if side == 0 else 1 - core) * per_dev

            @pl.loop(0, per_dev, unroll=min(4, per_dev))
            def _(local):
                one(side * per_dev + local, base, base + local)

    chunk = math.gcd(sites, 16)

    def sweep(body, count):
        def step(index, accs):
            return tuple(a + t for a, t in zip(accs, body(pl.ds(index * chunk, chunk))))

        accs = lax.fori_loop(0, sites // chunk, step, (jnp.zeros((rows, LANES), F32),) * count)
        return [fold(acc) for acc in accs]

    def fold(acc):
        total = jnp.sum(acc, axis=0, keepdims=True)
        total = jnp.broadcast_to(total, (rows, LANES))
        shift = half
        while shift < LANES:
            total = total + pltpu.roll(total, shift, 1)
            shift *= 2
        return total

    def dots(first, second):
        return jnp.sum(first * second, axis=0)

    def store_into(vec):
        def store(row, value):
            vec[me * block + row] = value

        return store

    gather(0, vec0, (prepare, prepare_other))
    (norm_sq,) = sweep(lambda s: (dots(vec0[s], vec0[s]),), 1)
    beta = jnp.sqrt(norm_sq)
    apply_op(vec0, beta, store_into(vec1))
    gather(1, vec1)
    (inner,) = sweep(lambda s: (dots(vec0[s], vec1[s]),), 1)
    h00 = inner / beta
    scale0 = h00 / beta

    def orthogonal1(s):
        left_over = vec1[s] - scale0 * vec0[s]
        vec1[s] = left_over
        return (dots(left_over, left_over),)

    (norm_sq,) = sweep(orthogonal1, 1)
    h10 = jnp.sqrt(norm_sq)

    apply_op(vec1, h10, store_into(vec2))
    gather(2, vec2)

    def inner2(s):
        image = vec2[s]
        return dots(vec0[s], image), dots(vec1[s], image)

    first, second = sweep(inner2, 2)
    h01, h11 = first / beta, second / h10
    scale0, scale1 = h01 / beta, h11 / h10

    def orthogonal2(s):
        left_over = vec2[s] - scale0 * vec0[s] - scale1 * vec1[s]
        vec2[s] = left_over
        return (dots(left_over, left_over),)

    (norm_sq,) = sweep(orthogonal2, 1)
    h21 = jnp.sqrt(norm_sq)

    def store_image(row, value):
        image_ref[row] = value

    apply_op(vec2, h21, store_image)
    mine = pl.ds(me * block, block)
    image = image_ref[...]
    for place, vec in enumerate((vec0, vec1, vec2)):
        parts[me, place * rows : (place + 1) * rows] = dots(vec[mine], image)
    parts[me, 3 * rows : 4 * rows] = dots(image, image)

    def part_copy(step, arriving):
        chip = lax.rem(me - step + chips, chips) if arriving else me
        ref = parts.at[chip]
        return remote(
            ref, ref, s_send.at[step], s_recv.at[step], chip_device(lax.rem(me + step, chips))
        )

    @pl.loop(1, chips)
    def _(step):
        part_copy(step, False).start()

    @pl.loop(1, chips)
    def _(step):
        part_copy(step, True).wait_recv()

    @pl.loop(1, chips)
    def _(step):
        part_copy(step, False).wait_send()

    summed = jnp.sum(parts[...], axis=0)
    sums = [fold(summed[place * rows : (place + 1) * rows]) for place in range(4)]
    h02, h12, h22 = sums[0] / beta, sums[1] / h10, sums[2] / h21

    g00 = h00 * h00 + h10 * h10
    g01 = h00 * h01 + h10 * h11
    g02 = h00 * h02 + h10 * h12
    g11 = h01 * h01 + h11 * h11 + h21 * h21
    g12 = h01 * h02 + h11 * h12 + h21 * h22
    g22 = sums[3]
    l00 = jnp.sqrt(g00)
    l10, l20 = g01 / l00, g02 / l00
    l11 = jnp.sqrt(g11 - l10 * l10)
    l21 = (g12 - l20 * l10) / l11
    l22 = jnp.sqrt(g22 - l20 * l20 - l21 * l21)
    t0 = beta * h00 / l00
    t1 = (beta * h01 - l10 * t0) / l11
    t2 = (beta * h02 - l20 * t0 - l21 * t1) / l22
    y2 = t2 / l22
    y1 = (t1 - l21 * y2) / l11
    y0 = (t0 - l10 * y1 - l20 * y2) / l00
    y0, y1, y2 = y0 / beta, y1 / h10, y2 / h21

    sent[...] = y0 * vec0[other_rows] + y1 * vec1[other_rows] + y2 * vec2[other_rows]
    swap = remote(sent, received, p_send.at[2], p_recv.at[2], partner)
    swap.start()
    out_ref[core] = y0 * vec0[own_rows] + y1 * vec1[own_rows] + y2 * vec2[own_rows]
    swap.wait()
    out_ref[1 - core] = received[...]


def per_device(coarse_op, right_side, owner_map, neighbor_table):
    subs, planes = lax.axis_size("sub"), lax.axis_size("grp") // 2
    per_dev, dof, width = coarse_op.shape
    rhs = right_side.shape[2]
    hops = width // dof - 1
    half = rhs // 2
    pack = LANES // half
    rows = dof // pack
    site_count = owner_map.shape[0]
    block = 2 * per_dev
    depth = (hops + 1) * rows

    slots = jnp.arange(site_count, dtype=jnp.int32)
    owner_block = slots // per_dev
    slot_grp, slot_sub = owner_block // subs, owner_block % subs
    place = ((slot_grp // 2 * subs + slot_sub) * 2 + slot_grp % 2) * per_dev + slots % per_dev
    place_of = jnp.sum(jnp.where(owner_map[None, :] == slots[:, None], place[None, :], 0), axis=1)

    packed = right_side.reshape(per_dev, pack, rows, 2, half).transpose(3, 0, 2, 1, 4)
    packed = packed.reshape(2, per_dev, rows, LANES)
    smem = pl.BlockSpec(memory_space=pltpu.SMEM)
    vmem = pl.BlockSpec(memory_space=pltpu.VMEM)
    keys = 2 * planes - 1
    dma = pltpu.SemaphoreType.DMA
    vector = pltpu.VMEM((site_count, rows, LANES), F32)
    small = pltpu.VMEM((per_dev, rows, LANES), F32)
    solved = pl.pallas_call(
        functools.partial(kernel, planes, subs, per_dev, dof, half, hops),
        out_shape=jax.ShapeDtypeStruct((2, per_dev, rows, LANES), F32),
        in_specs=[smem, smem, smem, vmem, vmem],
        out_specs=vmem,
        scratch_shapes=[
            vector,
            vector,
            vector,
            pltpu.VMEM((block, rows, LANES), F32),
            pltpu.VMEM((per_dev, dof, width), F32),
            pltpu.VMEM((block, pack * dof, depth), BF16),
            pltpu.VMEM((block, pack * dof, depth), BF16),
            pltpu.SMEM((block * hops,), jnp.int32),
            pltpu.VMEM((planes * subs, 4 * rows, LANES), F32),
            small,
            small,
            dma((3, 2, planes)),
            dma((3, 2, planes)),
            dma((3, keys, 2, subs // 2 + 1)),
            dma((3, keys, 2, subs // 2 + 1)),
            dma((3,)),
            dma((3,)),
            dma((planes * subs,)),
            dma((planes * subs,)),
            dma,
        ],
        compiler_params=pltpu.CompilerParams(
            collective_id=0, has_side_effects=True, vmem_limit_bytes=48 * 1024 * 1024
        ),
    )(place_of, neighbor_table.reshape(-1), owner_map, packed, coarse_op)
    solved = solved.reshape(2, per_dev, rows, pack, half).transpose(1, 3, 2, 0, 4)
    return solved.reshape(per_dev, dof, rhs)


def solution(mesh):
    placed = (P(("grp", "sub"), None, None), P(("grp", "sub"), None, None), P(), P())
    return jax.shard_map(
        per_device,
        mesh=mesh,
        in_specs=placed,
        out_specs=P(("grp", "sub"), None, None),
        check_vma=False,
    )
```

time: 309 us -> 94.2 us (0.30)
  blocking collectives: 135 us -> 0 us
  Pallas kernels: 0 us -> 89.8 us
  waiting for transfers between devices: 46.8 us -> 0 us
  matrix products: 42.5 us -> 0 us
  local copies, waits for them, and re-layouts: 42.9 us -> 3.89 us
  other arithmetic: 21.1 us -> 0.14 us
  between operations: 13.7 us -> 0.08 us
  starting transfers between devices: 6.36 us -> 0 us
    pallas_call x0 -> x1, Pallas kernels: none -> 89.8 us  [per_device(): pl.pallas_call(functools.partial(kernel, planes, subs, per_dev, dof, half...]
    psum x10 -> x0, blocking collectives: 89 us -> none  [reduce_sum(): return lax.psum(values, 'sub')]
    all_gather x1 -> x0, waiting for transfers between devices: 46.1 us -> none  [per_device(): op_rows = lax.all_gather(coarse_op, 'grp', axis=0, tiled=True)]
    dot_general x7 -> x0, matrix products: 42.5 us -> none  [the longest x3 38.9 us: per_device(): jnp.einsum('sac,scr->sar', op_rows, stacked, precision=lax.Precision.HIGH...]
    all_gather x3 -> x0, blocking collectives: 36.5 us -> none  [per_device(): piece = lax.all_gather(apply_vector, 'sub', axis=0, tiled=True)]
    gather x4 -> x0, local copies, waits for them, and re-layouts: 14.6 us -> none  [the longest x3 14 us: per_device(): link = inverse[neighbor_table[owner_map]]]
    concatenate x3 -> x0, local copies, waits for them, and re-layouts: 13 us -> none  [per_device(): jnp.concatenate([apply_vector[:, None], nearby], axis=1)]
    all_to_all x1 -> x0, blocking collectives: 9.14 us -> none  [per_device(): lax.all_to_all(solution, 'grp', split_axis=0, concat_axis=2, tiled=True)]
  transfers between devices with their start and end apart: 2 -> 0, of which waited for: 1 -> 0; matrix products, arithmetic and copies ran while one was open for 10% -> 0% of each run, Pallas kernels for 0% -> 0%
where the time goes in v1:
time: 94.2 us; the launch traced here: 94 us
  Pallas kernels  89.8 us (95%)
  local copies, waits for them, and re-layouts  3.89 us (4%)
    pallas_call x1, Pallas kernels, per_device(): pl.pallas_call(functools.partial(kernel, planes, subs, per_dev, dof, half...  89.8 us

profile of v1, /device:TPU:0, one launch (start us, length us, event | category | flops | bytes accessed | tf_op | source)
XLA Modules:
  0.0 94.0 jit_solution(17505818619934954339)
XLA Ops:
  0.0 0.0 copy-start.2
  0.0 0.0 copy-start.1
  0.0 0.0 copy-start
  0.0 1.4 %reshape.95 = f32[8,4,16,2,32]{4,3,2,1,0:T(2,128)S(1)} reshape(f32[8,64,64]{2,1,0:T(8,128)} %param.5) | data formatting | bytes 262144 | tf_op jit(solution)/shard_map/reshape | solution.py:415
  1.4 0.3 copy.14
  1.7 0.3 reshape.96.rhs_ref
  2.0 0.0 copy-done.2
  2.0 0.1 copy.10
  2.1 0.1 reshape.94.table_ref
  2.3 0.0 copy-done.1
  2.3 0.1 select_reduce_fusion.place_ref
  2.4 0.0 copy-done
  2.4 89.8 %shard_map.46 = f32[2,8,16,128]{3,2,1,0:T(8,128)S(1)} custom-call(s32[256]{0:T(256)S(1)} %select_reduce_fusion.place_ref, s32[2048]{0:T(1024)S(1)} %reshape.94.table_ref, s32[256]{0:T(256)S(1)} %copy-done.1, f32[2,8,16,128]{3,2,1,0:T(8,128)S(1)} %reshape.96.rhs_ref, f32[8,64,576]{2,1,0:T(8,128)S(1)} %copy-done), custom_call_target="tpu_custom_call" | custom-call | tf_op jit(solution)/shard_map/pallas_call | solution.py:423
  92.3 0.3 reshape.97
  92.5 0.4 copy.12
  92.9 1.0 %reshape.98 = f32[8,64,64]{2,1,0:T(8,128)} reshape(f32[8,4,16,2,32]{4,3,2,1,0:T(2,128)S(1)} %copy.12) | data formatting | bytes 262144 | tf_op jit(solution)/shard_map/reshape | solution.py:455
  (1 shorter events, 0.0 us)
Async XLA Ops:
  0.0 2.0 %copy-start.2 = (s32[256,8]{0,1:T(8,128)S(1)}, s32[256,8]{0,1:T(8,128)}, u32[]{:S(2)}) copy-start(s32[256,8]{0,1:T(8,128)} %param.7) | copy-start | bytes 24580
  0.0 2.3 %copy-start.1 = (s32[256]{0:T(256)S(1)}, s32[256]{0:T(256)}, u32[]{:S(2)}) copy-start(s32[256]{0:T(256)} %owner_ref.1) | copy-start | bytes 3076
  0.0 2.4 %copy-start = (f32[8,64,576]{2,1,0:T(8,128)S(1)}, f32[8,64,576]{2,1,0:T(8,128)}, u32[]{:S(2)}) copy-start(f32[8,64,576]{2,1,0:T(8,128)} %op_ref.1) | copy-start | bytes 3538948

commit v2 on v1

--- a/solution.py
+++ b/solution.py
@@ -39,9 +39,9 @@
 
 def kernel(
     planes, subs, per_dev, dof, half, hops,
-    place_ref, table_ref, owner_ref, rhs_ref, op_ref, out_ref,
-    vec0, vec1, vec2, image_ref, op_other, cp_high, cp_low, links, parts, sent, received,
-    z_send, z_recv, r_send, r_recv, p_send, p_recv, s_send, s_recv, local_sem,
+    place_ref, table_ref, owner_ref, rhs_ref, op_hbm, out_ref,
+    packed, vec0, vec1, vec2, image_ref, op_ref, op_other, cp_high, cp_low, links, parts, sent, received,
+    z_send, z_recv, r_send, r_recv, p_send, p_recv, s_send, s_recv, local_sem, load_sem,
 ):
     pack = LANES // half
     rows = dof // pack
@@ -64,16 +64,27 @@
     def chip_device(chip):
         return (chip // subs * 2 + core, lax.rem(chip, subs))
 
+    op_load = pltpu.make_async_copy(op_hbm, op_ref, load_sem)
+    op_load.start()
     barrier = pltpu.get_barrier_semaphore()
-    pl.semaphore_signal(barrier, inc=1, device_id=partner, device_id_type=MESH)
-
-    @pl.loop(1, chips)
-    def _(step):
-        pl.semaphore_signal(
-            barrier, inc=1, device_id=chip_device(lax.rem(me + step, chips)), device_id_type=MESH
-        )
-
-    pl.semaphore_wait(barrier, chips)
+
+    def greet(device):
+        pl.semaphore_signal(barrier, inc=1, device_id=device, device_id_type=MESH)
+
+    greet(partner)
+    if subs > 1:
+        greet((grp, right))
+        greet((grp, left))
+    pl.when(plane > 0)(lambda: greet(((plane - 1) * 2 + core, sub)))
+    pl.when(plane < planes - 1)(lambda: greet(((plane + 1) * 2 + core, sub)))
+    for side in (0, 1):
+        columns = [
+            rhs_ref[:, quarter * rows : (quarter + 1) * rows, side * half : (side + 1) * half]
+            for quarter in range(pack)
+        ]
+        packed[side] = jnp.concatenate(columns, axis=2)
+    ends = jnp.where(plane > 0, 1, 0) + jnp.where(plane < planes - 1, 1, 0)
+    pl.semaphore_wait(barrier, (3 if subs > 1 else 1) + ends)
 
     def remote(src, dst, send, recv, device):
         return pltpu.make_async_remote_copy(
@@ -82,130 +93,141 @@
 
     own_rows = pl.ds(me * block + core * per_dev, per_dev)
     other_rows = pl.ds(me * block + (1 - core) * per_dev, per_dev)
-    rhs_swap = remote(rhs_ref.at[1 - core], vec0.at[own_rows], p_send.at[0], p_recv.at[0], partner)
+    rhs_swap = remote(packed.at[1 - core], vec0.at[own_rows], p_send.at[0], p_recv.at[0], partner)
     rhs_swap.start()
     op_swap = remote(op_ref, op_other, p_send.at[1], p_recv.at[1], partner)
-    op_swap.start()
-    rhs_keep = pltpu.make_async_copy(rhs_ref.at[core], vec0.at[own_rows], local_sem)
+    rhs_keep = pltpu.make_async_copy(packed.at[core], vec0.at[own_rows], local_sem)
     rhs_keep.start()
     rhs_keep.wait()
     rhs_swap.wait()
 
-    full_steps = (subs - 1) // 2
     ring_steps = subs // 2
     keys = [(0, 0)] + [(way, dist) for dist in range(1, planes) for way in (0, 1)]
-
-    def gather(number, vec, meanwhile=None):
+    opposite = ring_sub(ring_steps)
+    reach = planes // 2 if ring_steps and subs % 2 == 0 else 0
+
+    def gather(number, vec, meanwhile=()):
         def at(chip_plane, chip_sub, piece=None):
             start = (chip_plane * subs + chip_sub) * block
             if piece is None:
                 return vec.at[pl.ds(start, block)]
             return vec.at[pl.ds(start + piece * per_dev, per_dev)]
 
-        def plane_of(key):
-            way, dist = key
+        def plane_of(way, dist):
             return plane - dist if way == 0 else plane + dist
 
-        def present(key):
-            way, dist = key
+        def present(way, dist):
             return plane >= dist if way == 0 else plane + dist < planes
 
-        def guarded(key, action):
+        def guarded(key, action, *more):
             if key[1] == 0:
-                action()
+                action(key, *more)
             else:
-                pl.when(present(key))(action)
-
-        def z_copy(way, dist):
-            src_plane = plane - (dist - 1) if way == 0 else plane + (dist - 1)
+                pl.when(present(*key))(lambda: action(key, *more))
+
+        def keys_at(dist):
+            return [key for key in keys if key[1] == dist]
+
+        def z_copy(stream, way, dist, arriving):
+            ref = at(plane_of(way, dist if arriving else dist - 1), opposite if stream else sub)
             next_plane = plane + 1 if way == 0 else plane - 1
-            ref = at(src_plane, sub)
             return remote(
-                ref, ref, z_send.at[number, way, dist], z_recv.at[number, way, dist],
+                ref, ref, z_send.at[number, stream, way, dist], z_recv.at[number, stream, way, dist],
                 (next_plane * 2 + core, sub),
             )
 
         def z_goes(way):
             return plane < planes - 1 if way == 0 else plane > 0
 
-        def z_arrival(key):
-            way, dist = key
-            ref = at(plane_of(key), sub)
-            return remote(
-                ref, ref, z_send.at[number, way, dist], z_recv.at[number, way, dist], (grp, sub)
-            )
+        def z_forward(stream, way, dist):
+            if dist <= (reach if stream else planes - 1):
+                pl.when(z_goes(way))(lambda: z_copy(stream, way, dist, False).start())
+
+        def z_arrive(key, stream):
+            z_copy(stream, *key, True).wait_recv()
+            z_forward(stream, key[0], key[1] + 1)
+
+        def steps_of(key):
+            return ring_steps - 1 if 1 <= key[1] <= reach else ring_steps
 
         def ring_copy(key, way, step, arriving):
             offset = step if arriving else step - 1
             src = ring_sub(-offset if way == 0 else offset)
             piece = way if 2 * step == subs else None
-            ref = at(plane_of(key), src, piece)
+            ref = at(plane_of(*key), src, piece)
             index = keys.index(key)
             return remote(
                 ref, ref, r_send.at[number, index, way, step], r_recv.at[number, index, way, step],
                 (grp, right if way == 0 else left),
             )
 
-        def z_forward(way, dist):
-            if dist < planes:
-                pl.when(z_goes(way))(lambda: z_copy(way, dist).start())
-
-        def ring_start(key, step):
-            if step <= ring_steps:
-                for way in (0, 1):
-                    ring_copy(key, way, step, False).start()
+        def ring_start(key):
+            if steps_of(key):
+                for way in (0, 1):
+                    ring_copy(key, way, 1, False).start()
 
         def ring_follow(key):
-            for step in range(1, ring_steps):
+            for step in range(1, steps_of(key)):
                 for way in (0, 1):
                     ring_copy(key, way, step, True).wait_recv()
                     ring_copy(key, way, step + 1, False).start()
 
         def ring_last(key):
-            if ring_steps:
-                for way in (0, 1):
-                    ring_copy(key, way, ring_steps, True).wait_recv()
-
-        def arrive(key):
-            def action():
-                z_arrival(key).wait_recv()
-                z_forward(key[0], key[1] + 1)
-                ring_start(key, 1)
-
-            guarded(key, action)
-
+            if steps_of(key):
+                for way in (0, 1):
+                    ring_copy(key, way, steps_of(key), True).wait_recv()
+
+        def ring_sends(key):
+            for step in range(1, steps_of(key) + 1):
+                for way in (0, 1):
+                    ring_copy(key, way, step, False).wait_send()
+
+        own = (0, 0)
         for way in (0, 1):
-            z_forward(way, 1)
-        ring_start((0, 0), 1)
-        if meanwhile is not None:
-            meanwhile[0]()
-        behind = [(0, 0)]
+            z_forward(0, way, 1)
+        ring_start(own)
+        for task in meanwhile[:1]:
+            task()
+        if planes == 1:
+            ring_follow(own)
+            ring_last(own)
+        across = list(range(1, reach + 1))
         for dist in range(1, planes):
-            now = [key for key in keys if key[1] == dist]
-            for key in now:
-                arrive(key)
-            for key in behind:
-                guarded(key, functools.partial(ring_follow, key))
-            behind = now
-            if meanwhile is not None and dist < len(meanwhile):
-                meanwhile[dist]()
-        for key in behind:
-            guarded(key, functools.partial(ring_follow, key))
+            for key in keys_at(dist):
+                guarded(key, z_arrive, 0)
+            if dist == 1:
+                ring_follow(own)
+            for key in keys_at(dist):
+                guarded(key, ring_start)
+            for key in keys_at(dist - 1) if dist > 1 else ():
+                guarded(key, ring_follow)
+            if dist == min(2, planes - 1):
+                ring_last(own)
+                for way in (0, 1):
+                    z_forward(1, way, 1)
+            elif dist > 2 and across:
+                for key in keys_at(across.pop(0)):
+                    guarded(key, z_arrive, 1)
+            for task in meanwhile[dist : dist + 1]:
+                task()
+        for key in keys_at(planes - 1) if planes > 1 else ():
+            guarded(key, ring_follow)
+        for dist in across:
+            for key in keys_at(dist):
+                guarded(key, z_arrive, 1)
+        for key in keys[1:]:
+            guarded(key, ring_last)
+
+        def z_sends(stream, way, dist):
+            goes = jnp.logical_and(z_goes(way), present(way, dist - 1))
+            pl.when(goes)(lambda: z_copy(stream, way, dist, False).wait_send())
+
+        for stream in (0, 1):
+            for dist in range(1, reach + 1 if stream else planes):
+                for way in (0, 1):
+                    z_sends(stream, way, dist)
         for key in keys:
-            guarded(key, functools.partial(ring_last, key))
-
-        for dist in range(1, planes):
-            for way in (0, 1):
-                goes = jnp.logical_and(z_goes(way), present((way, dist - 1)))
-                pl.when(goes)(lambda way=way, dist=dist: z_copy(way, dist).wait_send())
-
-        def ring_sends(key):
-            for step in range(1, ring_steps + 1):
-                for way in (0, 1):
-                    ring_copy(key, way, step, False).wait_send()
-
-        for key in keys:
-            guarded(key, functools.partial(ring_sends, key))
+            guarded(key, ring_sends)
 
     width = (hops + 1) * dof
     depth = (hops + 1) * rows
@@ -231,9 +253,11 @@
                 slot = (slot_grp * subs + sub) * per_dev + local
                 coarse = owner_ref[slot]
                 for hop in range(hops):
-                    links[(side * per_dev + local) * hops + hop] = place_ref[table_ref[coarse * hops + hop]]
+                    links[(side * per_dev + local) * hops + hop] = place_ref[table_ref[hop, coarse]]
 
     def prepare():
+        op_load.wait()
+        op_swap.start()
         find_links()
         regroup(op_ref, 0)
 
@@ -340,9 +364,12 @@
     apply_op(vec2, h21, store_image)
     mine = pl.ds(me * block, block)
     image = image_ref[...]
-    for place, vec in enumerate((vec0, vec1, vec2)):
-        parts[me, place * rows : (place + 1) * rows] = dots(vec[mine], image)
-    parts[me, 3 * rows : 4 * rows] = dots(image, image)
+    products = [dots(vec[mine], image) for vec in (vec0, vec1, vec2)] + [dots(image, image)]
+    at_row = lax.broadcasted_iota(jnp.int32, (8, LANES), 0)
+    part = jnp.zeros((8, LANES), F32)
+    for place, product in enumerate(products):
+        part = jnp.where(at_row == place, jnp.sum(product, axis=0, keepdims=True), part)
+    parts[me] = part
 
     def part_copy(step, arriving):
         chip = lax.rem(me - step + chips, chips) if arriving else me
@@ -364,7 +391,7 @@
         part_copy(step, False).wait_send()
 
     summed = jnp.sum(parts[...], axis=0)
-    sums = [fold(summed[place * rows : (place + 1) * rows]) for place in range(4)]
+    sums = [fold(summed[place : place + 1]) for place in range(4)]
     h02, h12, h22 = sums[0] / beta, sums[1] / h10, sums[2] / h21
 
     g00 = h00 * h00 + h10 * h10
@@ -389,9 +416,16 @@
     sent[...] = y0 * vec0[other_rows] + y1 * vec1[other_rows] + y2 * vec2[other_rows]
     swap = remote(sent, received, p_send.at[2], p_recv.at[2], partner)
     swap.start()
-    out_ref[core] = y0 * vec0[own_rows] + y1 * vec1[own_rows] + y2 * vec2[own_rows]
+    kept = y0 * vec0[own_rows] + y1 * vec1[own_rows] + y2 * vec2[own_rows]
     swap.wait()
-    out_ref[1 - core] = received[...]
+    came = received[...]
+    first = jnp.where(core == 0, kept, came)
+    second = jnp.where(core == 0, came, kept)
+    for quarter in range(pack):
+        lanes = slice(quarter * half, (quarter + 1) * half)
+        out_ref[:, quarter * rows : (quarter + 1) * rows, :] = jnp.concatenate(
+            [first[:, :, lanes], second[:, :, lanes]], axis=2
+        )
 
 
 def per_device(coarse_op, right_side, owner_map, neighbor_table):
@@ -412,33 +446,33 @@
     place = ((slot_grp // 2 * subs + slot_sub) * 2 + slot_grp % 2) * per_dev + slots % per_dev
     place_of = jnp.sum(jnp.where(owner_map[None, :] == slots[:, None], place[None, :], 0), axis=1)
 
-    packed = right_side.reshape(per_dev, pack, rows, 2, half).transpose(3, 0, 2, 1, 4)
-    packed = packed.reshape(2, per_dev, rows, LANES)
     smem = pl.BlockSpec(memory_space=pltpu.SMEM)
     vmem = pl.BlockSpec(memory_space=pltpu.VMEM)
     keys = 2 * planes - 1
     dma = pltpu.SemaphoreType.DMA
     vector = pltpu.VMEM((site_count, rows, LANES), F32)
     small = pltpu.VMEM((per_dev, rows, LANES), F32)
-    solved = pl.pallas_call(
+    return pl.pallas_call(
         functools.partial(kernel, planes, subs, per_dev, dof, half, hops),
-        out_shape=jax.ShapeDtypeStruct((2, per_dev, rows, LANES), F32),
-        in_specs=[smem, smem, smem, vmem, vmem],
+        out_shape=jax.ShapeDtypeStruct(right_side.shape, F32),
+        in_specs=[smem, smem, smem, vmem, pl.BlockSpec(memory_space=pl.ANY)],
         out_specs=vmem,
         scratch_shapes=[
+            pltpu.VMEM((2, per_dev, rows, LANES), F32),
             vector,
             vector,
             vector,
             pltpu.VMEM((block, rows, LANES), F32),
             pltpu.VMEM((per_dev, dof, width), F32),
+            pltpu.VMEM((per_dev, dof, width), F32),
             pltpu.VMEM((block, pack * dof, depth), BF16),
             pltpu.VMEM((block, pack * dof, depth), BF16),
             pltpu.SMEM((block * hops,), jnp.int32),
-            pltpu.VMEM((planes * subs, 4 * rows, LANES), F32),
+            pltpu.VMEM((planes * subs, 8, LANES), F32),
             small,
             small,
-            dma((3, 2, planes)),
-            dma((3, 2, planes)),
+            dma((3, 2, 2, planes)),
+            dma((3, 2, 2, planes)),
             dma((3, keys, 2, subs // 2 + 1)),
             dma((3, keys, 2, subs // 2 + 1)),
             dma((3,)),
@@ -446,13 +480,12 @@
             dma((planes * subs,)),
             dma((planes * subs,)),
             dma,
+            dma,
         ],
         compiler_params=pltpu.CompilerParams(
             collective_id=0, has_side_effects=True, vmem_limit_bytes=48 * 1024 * 1024
         ),
-    )(place_of, neighbor_table.reshape(-1), owner_map, packed, coarse_op)
-    solved = solved.reshape(2, per_dev, rows, pack, half).transpose(1, 3, 2, 0, 4)
-    return solved.reshape(per_dev, dof, rhs)
+    )(place_of, neighbor_table.T, owner_map, right_side, coarse_op)
 
 
 def solution(mesh):

time: 94.2 us -> 92 us (0.977)
  Pallas kernels: 89.8 us -> 86.6 us
    unnamed x7 -> x9, local copies, waits for them, and re-layouts: 0.13 us -> 4.34 us
    reshape x6 -> x0, local copies, waits for them, and re-layouts: 3.35 us -> none  [the longest x2 1.71 us: per_device(): right_side.reshape(per_dev, pack, rows, 2, half).transpose(3, 0, 2, 1, 4)]
    pallas_call x1, Pallas kernels: 89.8 us -> 86.6 us  [per_device(): pl.pallas_call(functools.partial(kernel, planes, subs, per_dev, dof, half...]
where the time goes in v2:
time: 92 us; the launch traced here: 91.8 us
  Pallas kernels  86.6 us (94%)
  local copies, waits for them, and re-layouts  4.34 us (5%)
    pallas_call x1, Pallas kernels, per_device(): pl.pallas_call(functools.partial(kernel, planes, subs, per_dev, dof, half...  86.6 us
    unnamed x9, local copies, waits for them, and re-layouts  4.34 us

profile of v2, /device:TPU:0, one launch (start us, length us, event | category | flops | bytes accessed | tf_op | source)
XLA Modules:
  0.0 91.8 jit_solution(16149968267732423317)
XLA Ops:
  0.0 0.8 select_reduce_fusion.place_ref
  0.8 0.0 copy-start
  0.8 1.3 %copy-done = f32[8,64,576]{2,1,0:T(8,128)S(1)} copy-done((f32[8,64,576]{2,1,0:T(8,128)S(1)}, f32[8,64,576]{2,1,0:T(8,128)}, u32[]{:S(2)}) %copy-start) | copy-done | bytes 1179672
  2.1 0.0 copy-start.1
  2.1 0.9 %copy-done.1 = f32[8,64,64]{2,1,0:T(8,128)S(1)} copy-done((f32[8,64,64]{2,1,0:T(8,128)S(1)}, f32[8,64,64]{2,1,0:T(8,128)}, u32[]{:S(2)}) %copy-start.1) | copy-done | bytes 131096
  3.1 0.0 copy-start.2
  3.1 0.7 copy-done.2
  3.8 0.0 copy-start.3
  3.8 0.7 copy-done.3
  4.5 86.6 %shard_map.46 = f32[8,64,64]{2,1,0:T(8,128)S(1)} custom-call(s32[256]{0:T(256)S(1)} %select_reduce_fusion.place_ref, s32[8,256]{1,0:T(8,128)S(1)} %bitcast.1, s32[256]{0:T(256)S(1)} %copy-done.3, f32[8,64,64]{2,1,0:T(8,128)S(1)} %copy-done.1, f32[8,64,576]{2,1,0:T(8,128)S(1)} %copy-done), custom_call_target="tpu_custom_call" | custom-call | tf_op jit(solution)/shard_map/pallas_call | solution.py:455
  91.1 0.7 copy.6
  (1 shorter events, 0.0 us)
Async XLA Ops:
  0.8 1.3 %copy-start = (f32[8,64,576]{2,1,0:T(8,128)S(1)}, f32[8,64,576]{2,1,0:T(8,128)}, u32[]{:S(2)}) copy-start(f32[8,64,576]{2,1,0:T(8,128)} %op_hbm.1) | copy-start | bytes 3538948
  2.1 0.9 %copy-start.1 = (f32[8,64,64]{2,1,0:T(8,128)S(1)}, f32[8,64,64]{2,1,0:T(8,128)}, u32[]{:S(2)}) copy-start(f32[8,64,64]{2,1,0:T(8,128)} %rhs_ref.1) | copy-start | bytes 393220
  3.1 0.7 copy-start.2
  3.8 0.7 copy-start.3

commit v3 on v2

--- a/solution.py
+++ b/solution.py
@@ -98,20 +98,19 @@
     op_swap = remote(op_ref, op_other, p_send.at[1], p_recv.at[1], partner)
     rhs_keep = pltpu.make_async_copy(packed.at[core], vec0.at[own_rows], local_sem)
     rhs_keep.start()
-    rhs_keep.wait()
-    rhs_swap.wait()
 
     ring_steps = subs // 2
     keys = [(0, 0)] + [(way, dist) for dist in range(1, planes) for way in (0, 1)]
     opposite = ring_sub(ring_steps)
-    reach = planes // 2 if ring_steps and subs % 2 == 0 else 0
-
-    def gather(number, vec, meanwhile=()):
-        def at(chip_plane, chip_sub, piece=None):
-            start = (chip_plane * subs + chip_sub) * block
-            if piece is None:
-                return vec.at[pl.ds(start, block)]
-            return vec.at[pl.ds(start + piece * per_dev, per_dev)]
+    reach = (planes - 1) // 2 if ring_steps and subs % 2 == 0 else 0
+
+    halves = (0, 1)
+    ways = (0, 1)
+
+    def gathering(number, vec):
+        def at(chip_plane, chip_sub, piece):
+            first = core if piece == 0 else 1 - core
+            return vec.at[pl.ds((chip_plane * subs + chip_sub) * block + first * per_dev, per_dev)]
 
         def plane_of(way, dist):
             return plane - dist if way == 0 else plane + dist
@@ -128,106 +127,120 @@
         def keys_at(dist):
             return [key for key in keys if key[1] == dist]
 
-        def z_copy(stream, way, dist, arriving):
-            ref = at(plane_of(way, dist if arriving else dist - 1), opposite if stream else sub)
+        def z_copy(stream, way, dist, piece, arriving):
+            ref = at(plane_of(way, dist if arriving else dist - 1), opposite if stream else sub, piece)
             next_plane = plane + 1 if way == 0 else plane - 1
-            return remote(
-                ref, ref, z_send.at[number, stream, way, dist], z_recv.at[number, stream, way, dist],
-                (next_plane * 2 + core, sub),
-            )
+            index = (number, stream, way, dist - 1, piece)
+            return remote(ref, ref, z_send.at[index], z_recv.at[index], (next_plane * 2 + core, sub))
 
         def z_goes(way):
             return plane < planes - 1 if way == 0 else plane > 0
 
-        def z_forward(stream, way, dist):
+        def z_forward(stream, way, dist, piece):
             if dist <= (reach if stream else planes - 1):
-                pl.when(z_goes(way))(lambda: z_copy(stream, way, dist, False).start())
-
-        def z_arrive(key, stream):
-            z_copy(stream, *key, True).wait_recv()
-            z_forward(stream, key[0], key[1] + 1)
-
-        def steps_of(key):
-            return ring_steps - 1 if 1 <= key[1] <= reach else ring_steps
-
-        def ring_copy(key, way, step, arriving):
+                pl.when(z_goes(way))(lambda: z_copy(stream, way, dist, piece, False).start())
+
+        def z_arrive(key, stream, piece):
+            z_copy(stream, *key, piece, True).wait_recv()
+            z_forward(stream, key[0], key[1] + 1, piece)
+
+        def ring_moves(key):
+            steps = ring_steps - 1 if 1 <= key[1] <= reach else ring_steps
+            return [
+                [(way, piece) for way in ways for piece in (way, 1 - way) if 2 * step != subs or piece == way]
+                for step in range(1, steps + 1)
+            ]
+
+        def ring_copy(key, step, way, piece, arriving):
             offset = step if arriving else step - 1
-            src = ring_sub(-offset if way == 0 else offset)
-            piece = way if 2 * step == subs else None
-            ref = at(plane_of(*key), src, piece)
-            index = keys.index(key)
+            ref = at(plane_of(*key), ring_sub(-offset if way == 0 else offset), piece)
+            index = (number, keys.index(key), way, step - 1, piece)
             return remote(
-                ref, ref, r_send.at[number, index, way, step], r_recv.at[number, index, way, step],
-                (grp, right if way == 0 else left),
+                ref, ref, r_send.at[index], r_recv.at[index], (grp, right if way == 0 else left)
             )
 
-        def ring_start(key):
-            if steps_of(key):
-                for way in (0, 1):
-                    ring_copy(key, way, 1, False).start()
+        def ring_start(key, pieces=halves):
+            for way, piece in (ring_moves(key) or [[]])[0]:
+                if piece in pieces:
+                    ring_copy(key, 1, way, piece, False).start()
 
         def ring_follow(key):
-            for step in range(1, steps_of(key)):
-                for way in (0, 1):
-                    ring_copy(key, way, step, True).wait_recv()
-                    ring_copy(key, way, step + 1, False).start()
+            moves = ring_moves(key)
+            for step in range(2, len(moves) + 1):
+                for way, piece in moves[step - 1]:
+                    ring_copy(key, step - 1, way, piece, True).wait_recv()
+                    ring_copy(key, step, way, piece, False).start()
 
         def ring_last(key):
-            if steps_of(key):
-                for way in (0, 1):
-                    ring_copy(key, way, steps_of(key), True).wait_recv()
+            moves = ring_moves(key)
+            for step in range(1, len(moves) + 1):
+                for way, piece in moves[step - 1]:
+                    if step == len(moves) or (way, piece) not in moves[step]:
+                        ring_copy(key, step, way, piece, True).wait_recv()
 
         def ring_sends(key):
-            for step in range(1, steps_of(key) + 1):
-                for way in (0, 1):
-                    ring_copy(key, way, step, False).wait_send()
+            for step, moves in enumerate(ring_moves(key)):
+                for way, piece in moves:
+                    ring_copy(key, step + 1, way, piece, False).wait_send()
 
         own = (0, 0)
-        for way in (0, 1):
-            z_forward(0, way, 1)
-        ring_start(own)
-        for task in meanwhile[:1]:
-            task()
-        if planes == 1:
-            ring_follow(own)
-            ring_last(own)
-        across = list(range(1, reach + 1))
-        for dist in range(1, planes):
-            for key in keys_at(dist):
-                guarded(key, z_arrive, 0)
-            if dist == 1:
+
+        def begin(piece):
+            for way in ways:
+                z_forward(0, way, 1, piece)
+            ring_start(own, (piece,))
+
+        def finish(meanwhile=()):
+            for task in meanwhile[:1]:
+                task()
+            if planes == 1:
                 ring_follow(own)
-            for key in keys_at(dist):
-                guarded(key, ring_start)
-            for key in keys_at(dist - 1) if dist > 1 else ():
+                ring_last(own)
+            across = list(range(1, reach + 1))
+            for dist in range(1, planes):
+                for piece in halves:
+                    for key in keys_at(dist):
+                        guarded(key, z_arrive, 0, piece)
+                    if dist == 1 and piece == 0:
+                        ring_follow(own)
+                for key in keys_at(dist):
+                    guarded(key, ring_start)
+                for key in keys_at(dist - 1) if dist > 1 else ():
+                    guarded(key, ring_follow)
+                if dist == min(2, planes - 1):
+                    ring_last(own)
+                    for piece in halves:
+                        for way in ways:
+                            z_forward(1, way, 1, piece)
+                elif dist > 2 and across:
+                    pair = across.pop(0)
+                    for piece in halves:
+                        for key in keys_at(pair):
+                            guarded(key, z_arrive, 1, piece)
+                for task in meanwhile[dist : dist + 1]:
+                    task()
+            for key in keys_at(planes - 1) if planes > 1 else ():
                 guarded(key, ring_follow)
-            if dist == min(2, planes - 1):
-                ring_last(own)
-                for way in (0, 1):
-                    z_forward(1, way, 1)
-            elif dist > 2 and across:
-                for key in keys_at(across.pop(0)):
-                    guarded(key, z_arrive, 1)
-            for task in meanwhile[dist : dist + 1]:
-                task()
-        for key in keys_at(planes - 1) if planes > 1 else ():
-            guarded(key, ring_follow)
-        for dist in across:
-            for key in keys_at(dist):
-                guarded(key, z_arrive, 1)
-        for key in keys[1:]:
-            guarded(key, ring_last)
-
-        def z_sends(stream, way, dist):
-            goes = jnp.logical_and(z_goes(way), present(way, dist - 1))
-            pl.when(goes)(lambda: z_copy(stream, way, dist, False).wait_send())
-
-        for stream in (0, 1):
-            for dist in range(1, reach + 1 if stream else planes):
-                for way in (0, 1):
-                    z_sends(stream, way, dist)
-        for key in keys:
-            guarded(key, ring_sends)
+            for dist in across:
+                for piece in halves:
+                    for key in keys_at(dist):
+                        guarded(key, z_arrive, 1, piece)
+            for key in keys[1:]:
+                guarded(key, ring_last)
+
+            def z_sends(stream, way, dist, piece):
+                goes = jnp.logical_and(z_goes(way), present(way, dist - 1))
+                pl.when(goes)(lambda: z_copy(stream, way, dist, piece, False).wait_send())
+
+            for stream in (0, 1):
+                for dist in range(1, reach + 1 if stream else planes):
+                    for way in ways:
+                        for piece in halves:
+                            z_sends(stream, way, dist, piece)
+            for key in keys:
+                guarded(key, ring_sends)
+
+        return begin, finish
 
     width = (hops + 1) * dof
     depth = (hops + 1) * rows
@@ -267,8 +280,8 @@
 
     lane_group = lax.broadcasted_iota(jnp.int32, (rows, LANES), 1) // half
 
-    def apply_op(vec, over, store):
-        def one(index, base, count_row):
+    def apply_op(vec, over, store, then=None):
+        def one(index, count_row):
             own = me * block + count_row
             pieces = [vec[own]] + [vec[links[index * hops + hop]] for hop in range(hops)]
             high, low = split(jnp.concatenate(pieces, axis=0))
@@ -293,7 +306,10 @@
 
             @pl.loop(0, per_dev, unroll=min(4, per_dev))
             def _(local):
-                one(side * per_dev + local, base, base + local)
+                one(side * per_dev + local, base + local)
+
+            if then is not None:
+                then(side)
 
     chunk = math.gcd(sites, 16)
 
@@ -322,11 +338,17 @@
 
         return store
 
-    gather(0, vec0, (prepare, prepare_other))
+    begin, finish = gathering(0, vec0)
+    rhs_keep.wait()
+    begin(0)
+    rhs_swap.wait()
+    begin(1)
+    finish((prepare, prepare_other))
     (norm_sq,) = sweep(lambda s: (dots(vec0[s], vec0[s]),), 1)
     beta = jnp.sqrt(norm_sq)
-    apply_op(vec0, beta, store_into(vec1))
-    gather(1, vec1)
+    begin, finish = gathering(1, vec1)
+    apply_op(vec0, beta, store_into(vec1), begin)
+    finish()
     (inner,) = sweep(lambda s: (dots(vec0[s], vec1[s]),), 1)
     h00 = inner / beta
     scale0 = h00 / beta
@@ -339,8 +361,9 @@
     (norm_sq,) = sweep(orthogonal1, 1)
     h10 = jnp.sqrt(norm_sq)
 
-    apply_op(vec1, h10, store_into(vec2))
-    gather(2, vec2)
+    begin, finish = gathering(2, vec2)
+    apply_op(vec1, h10, store_into(vec2), begin)
+    finish()
 
     def inner2(s):
         image = vec2[s]
@@ -471,10 +494,10 @@
             pltpu.VMEM((planes * subs, 8, LANES), F32),
             small,
             small,
-            dma((3, 2, 2, planes)),
-            dma((3, 2, 2, planes)),
-            dma((3, keys, 2, subs // 2 + 1)),
-            dma((3, keys, 2, subs // 2 + 1)),
+            dma((3, 2, 2, max(planes - 1, 1), 2)),
+            dma((3, 2, 2, max(planes - 1, 1), 2)),
+            dma((3, keys, 2, max(subs // 2, 1), 2)),
+            dma((3, keys, 2, max(subs // 2, 1), 2)),
             dma((3,)),
             dma((3,)),
             dma((planes * subs,)),

time: 92 us -> 84.8 us (0.922)
  Pallas kernels: 86.6 us -> 79.4 us
    pallas_call x1, Pallas kernels: 86.6 us -> 79.4 us  [per_device(): pl.pallas_call(functools.partial(kernel, planes, subs, per_dev, dof, half...]
where the time goes in v3:
time: 84.8 us; the launch traced here: 84.6 us
  Pallas kernels  79.4 us (94%)
  local copies, waits for them, and re-layouts  4.34 us (5%)
    pallas_call x1, Pallas kernels, per_device(): pl.pallas_call(functools.partial(kernel, planes, subs, per_dev, dof, half...  79.4 us
    unnamed x9, local copies, waits for them, and re-layouts  4.34 us

profile of v3, /device:TPU:0, one launch (start us, length us, event | category | flops | bytes accessed | tf_op | source)
XLA Modules:
  0.0 84.6 jit_solution(4796066429936696442)
XLA Ops:
  0.0 0.8 select_reduce_fusion.place_ref
  0.8 0.0 copy-start
  0.8 1.3 %copy-done = f32[8,64,576]{2,1,0:T(8,128)S(1)} copy-done((f32[8,64,576]{2,1,0:T(8,128)S(1)}, f32[8,64,576]{2,1,0:T(8,128)}, u32[]{:S(2)}) %copy-start) | copy-done | bytes 1179672
  2.1 0.0 copy-start.1
  2.1 0.9 %copy-done.1 = f32[8,64,64]{2,1,0:T(8,128)S(1)} copy-done((f32[8,64,64]{2,1,0:T(8,128)S(1)}, f32[8,64,64]{2,1,0:T(8,128)}, u32[]{:S(2)}) %copy-start.1) | copy-done | bytes 131096
  3.1 0.0 copy-start.2
  3.1 0.7 copy-done.2
  3.8 0.0 copy-start.3
  3.8 0.7 copy-done.3
  4.5 79.4 %shard_map.46 = f32[8,64,64]{2,1,0:T(8,128)S(1)} custom-call(s32[256]{0:T(256)S(1)} %select_reduce_fusion.place_ref, s32[8,256]{1,0:T(8,128)S(1)} %bitcast.1, s32[256]{0:T(256)S(1)} %copy-done.3, f32[8,64,64]{2,1,0:T(8,128)S(1)} %copy-done.1, f32[8,64,576]{2,1,0:T(8,128)S(1)} %copy-done), custom_call_target="tpu_custom_call" | custom-call | tf_op jit(solution)/shard_map/pallas_call | solution.py:478
  83.9 0.7 copy.6
  (1 shorter events, 0.0 us)
Async XLA Ops:
  0.8 1.3 %copy-start = (f32[8,64,576]{2,1,0:T(8,128)S(1)}, f32[8,64,576]{2,1,0:T(8,128)}, u32[]{:S(2)}) copy-start(f32[8,64,576]{2,1,0:T(8,128)} %op_hbm.1) | copy-start | bytes 3538948
  2.1 0.9 %copy-start.1 = (f32[8,64,64]{2,1,0:T(8,128)S(1)}, f32[8,64,64]{2,1,0:T(8,128)}, u32[]{:S(2)}) copy-start(f32[8,64,64]{2,1,0:T(8,128)} %rhs_ref.1) | copy-start | bytes 393220
  3.1 0.7 copy-start.2
  3.8 0.7 copy-start.3

commit v4 on v3

--- a/solution.py
+++ b/solution.py
@@ -39,8 +39,8 @@
 
 def kernel(
     planes, subs, per_dev, dof, half, hops,
-    place_ref, table_ref, owner_ref, rhs_ref, op_hbm, out_ref,
-    packed, vec0, vec1, vec2, image_ref, op_ref, op_other, cp_high, cp_low, links, parts, sent, received,
+    place_ref, table_hbm, owner_hbm, rhs_hbm, op_hbm, out_ref,
+    table_ref, owner_ref, rhs_ref, packed, vec0, vec1, vec2, image_ref, op_ref, op_other, cp_high, cp_low, links, parts, sent, received,
     z_send, z_recv, r_send, r_recv, p_send, p_recv, s_send, s_recv, local_sem, load_sem,
 ):
     pack = LANES // half
@@ -64,8 +64,15 @@
     def chip_device(chip):
         return (chip // subs * 2 + core, lax.rem(chip, subs))
 
-    op_load = pltpu.make_async_copy(op_hbm, op_ref, load_sem)
-    op_load.start()
+    def load(source, kept, place):
+        copy = pltpu.make_async_copy(source, kept, load_sem.at[place])
+        copy.start()
+        return copy
+
+    rhs_load = load(rhs_hbm, rhs_ref, 0)
+    op_load = load(op_hbm, op_ref, 1)
+    table_load = load(table_hbm, table_ref, 2)
+    owner_load = load(owner_hbm, owner_ref, 3)
     barrier = pltpu.get_barrier_semaphore()
 
     def greet(device):
@@ -77,6 +84,7 @@
         greet((grp, left))
     pl.when(plane > 0)(lambda: greet(((plane - 1) * 2 + core, sub)))
     pl.when(plane < planes - 1)(lambda: greet(((plane + 1) * 2 + core, sub)))
+    rhs_load.wait()
     for side in (0, 1):
         columns = [
             rhs_ref[:, quarter * rows : (quarter + 1) * rows, side * half : (side + 1) * half]
@@ -259,6 +267,9 @@
                 )
 
     def find_links():
+        table_load.wait()
+        owner_load.wait()
+
         @pl.loop(0, per_dev)
         def _(local):
             for side in (0, 1):
@@ -478,9 +489,12 @@
     return pl.pallas_call(
         functools.partial(kernel, planes, subs, per_dev, dof, half, hops),
         out_shape=jax.ShapeDtypeStruct(right_side.shape, F32),
-        in_specs=[smem, smem, smem, vmem, pl.BlockSpec(memory_space=pl.ANY)],
+        in_specs=[smem] + [pl.BlockSpec(memory_space=pltpu.HBM)] * 4,
         out_specs=vmem,
         scratch_shapes=[
+            pltpu.SMEM((hops, site_count), jnp.int32),
+            pltpu.SMEM((site_count,), jnp.int32),
+            pltpu.VMEM(right_side.shape, F32),
             pltpu.VMEM((2, per_dev, rows, LANES), F32),
             vector,
             vector,
@@ -503,10 +517,10 @@
             dma((planes * subs,)),
             dma((planes * subs,)),
             dma,
-            dma,
+            dma((4,)),
         ],
         compiler_params=pltpu.CompilerParams(
-            collective_id=0, has_side_effects=True, vmem_limit_bytes=48 * 1024 * 1024
+            collective_id=0, has_side_effects=True, vmem_limit_bytes=67043328
         ),
     )(place_of, neighbor_table.T, owner_map, right_side, coarse_op)
 

time: 84.8 us -> 83.4 us (0.983)
  local copies, waits for them, and re-layouts: 4.34 us -> 1.67 us
    unnamed x9 -> x1, local copies, waits for them, and re-layouts: 4.34 us -> 1.67 us
where the time goes in v4:
time: 83.4 us; the launch traced here: 83.2 us
  Pallas kernels  80.1 us (96%)
  local copies, waits for them, and re-layouts  1.67 us (2%)
  other arithmetic  1.38 us (2%)
    pallas_call x1, Pallas kernels, per_device(): pl.pallas_call(functools.partial(kernel, planes, subs, per_dev, dof, half...  80.1 us
    unnamed x1, local copies, waits for them, and re-layouts  1.67 us

profile of v4, /device:TPU:0, one launch (start us, length us, event | category | flops | bytes accessed | tf_op | source)
XLA Modules:
  0.0 83.2 jit_solution(16211523316364123478)
XLA Ops:
  0.0 1.4 %select_reduce_fusion.place_ref = s32[256]{0:T(256)} fusion(s32[256]{0:T(256)S(1)} %fusion.2, s32[256]{0:T(256)} %owner_hbm.1), kind=kLoop, calls=%fused_computation | loop fusion | flops 196352 | bytes 3072 | tf_op jit(solution)/shard_map/reduce_sum | solution.py:481
  1.4 80.1 %shard_map.46 = f32[8,64,64]{2,1,0:T(8,128)} custom-call(s32[256]{0:T(256)} %select_reduce_fusion.place_ref, s32[8,256]{1,0:T(8,128)} %bitcast.1, s32[256]{0:T(256)} %owner_hbm.1, f32[8,64,64]{2,1,0:T(8,128)} %rhs_hbm.1, f32[8,64,576]{2,1,0:T(8,128)} %op_hbm.1), custom_call_target="tpu_custom_call" | custom-call | tf_op jit(solution)/shard_map/pallas_call | solution.py:489
  81.5 1.7 %copy.6 = f32[8,64,64]{2,1,0:T(8,128)} copy(f32[8,64,64]{2,1,0:T(8,128)} %shard_map.46) | data formatting | bytes 262144
  (1 shorter events, 0.0 us)
